TPU v7x, 32 devices: a whole 2x2x4 slice. The times are simulated.
32 devices in a mesh: rep: 4 (over x, core), tp: 8 (over z, y).
Axes of the slice: x: 2, y: 2, z: 4, core: 2. Of those that a mesh axis runs over, the one named last changes fastest.
Arguments:
- trainer_query: float32 [32, 256, 8192], P(('rep', 'tp')), may hold values from -6 to 6
- trainer_output: float32 [32, 8192, 256], P(('rep', 'tp')), may hold values from -6 to 6
- probes: bfloat16 [768, 8192], replicated, may hold values from -0.0625 to 0.0625
- shard_block: int32 [32], replicated, may hold values from 0 to 31, each once
- slice_owner: int32 [8], replicated, may hold values from 0 to 7, each once
Outputs:
- query_slices: bfloat16 [8, 8192, 1024], P('tp')
- output_slices: bfloat16 [8, 1024, 8192], P('tp')
- query_prints: float32 [8, 768, 1024], P('tp')
- output_prints: float32 [8, 1024, 768], P('tp')
Inputs may be any that keep to these rules, and one draw needn't show every extreme that they name: `shard_block`: a permutation: each number once. `slice_owner`: a permutation: each number once.
All inputs are finite; a program needn't handle non-finite values.
Results may differ from a plain program's by a relative error of at most 0.0029.
Values may be sent and summed in bfloat16 or wider, within the bound.
A program may use at most 192 MiB of HBM per device.

v0:
```python
import functools

import jax
import jax.numpy as jnp
from jax import lax
from jax.experimental import pallas as pl
from jax.experimental.pallas import tpu as pltpu
from jax.sharding import PartitionSpec as P

MESH = pl.DeviceIdType.MESH


def pack_kernel(owner_ref, query_ref, output_ref, query_blocks, output_blocks):
    query_blocks[...] = query_ref[...].astype(jnp.bfloat16)
    output_blocks[...] = output_ref[...].astype(jnp.bfloat16)


def pack(trainer_query, trainer_output, slice_owner):
    tp_count = slice_owner.shape[0]
    _, rows, width = trainer_query.shape
    cut = width // tp_count
    return pl.pallas_call(
        pack_kernel,
        out_shape=(
            jax.ShapeDtypeStruct((tp_count, rows, cut), jnp.bfloat16),
            jax.ShapeDtypeStruct((tp_count, cut, rows), jnp.bfloat16),
        ),
        grid_spec=pltpu.PrefetchScalarGridSpec(
            num_scalar_prefetch=1,
            grid=(tp_count,),
            in_specs=[
                pl.BlockSpec((1, rows, cut), lambda k, owner: (0, 0, owner[k])),
                pl.BlockSpec((1, cut, rows), lambda k, owner: (0, owner[k], 0)),
            ],
            out_specs=[
                pl.BlockSpec((1, rows, cut), lambda k, owner: (k, 0, 0)),
                pl.BlockSpec((1, cut, rows), lambda k, owner: (k, 0, 0)),
            ],
        ),
    )(slice_owner, trainer_query, trainer_output)


def pair_index(index, offset, count):
    paired, bit = 0, 1
    while bit < count:
        low = lax.rem(lax.div(index, bit) + lax.div(offset, bit), 2)
        paired = paired + bit * low
        bit *= 2
    return paired


def move_kernel(rep_count, tp_count, multiply, *refs):
    if multiply:
        (owner_ref, query_blocks, output_blocks, probes_ref,
         query_all, output_all, query_prints, output_prints,
         swap_send, swap_recv, near_send, near_recv, far_send, far_recv, own_sem,
         probes, picked, query_tile, output_tile, load_sem, probes_sem) = refs
    else:
        (query_blocks, output_blocks, query_all, output_all,
         swap_send, swap_recv, near_send, near_recv, far_send, far_recv, own_sem) = refs
    rep, tp = lax.axis_index("rep"), lax.axis_index("tp")
    partner = rep + 1 - 2 * lax.rem(rep, 2)
    hops = range(1, rep_count // 2)
    ahead = {hop: lax.rem(rep + 2 * hop, rep_count) for hop in hops}
    behind = {hop: lax.rem(rep + rep_count - 2 * hop, rep_count) for hop in hops}
    across = {hop: lax.rem(partner + rep_count - 2 * hop, rep_count) for hop in hops}
    arrays = ((query_blocks, query_all), (output_blocks, output_all))
    mine = rep * tp_count + tp
    count = rep_count * tp_count
    rows = query_blocks.shape[1]

    def load_probes(block):
        columns = pl.ds(pl.multiple_of(block * rows, rows), rows)
        return pltpu.make_async_copy(
            probes_ref.at[:, columns], probes.at[block], probes_sem.at[block]
        )

    def pair(offset):
        return pair_index(tp, jnp.int32(offset), tp_count)

    barrier = pltpu.get_barrier_semaphore()
    peers = [(rep, pair(offset)) for offset in range(1, tp_count)]
    peers += [(partner, tp)] + [(ahead[hop], tp) for hop in hops]
    for peer in peers:
        pl.semaphore_signal(barrier, inc=1, device_id=peer, device_id_type=MESH)
    pl.semaphore_wait(barrier, len(peers))

    def remote(source, target, send_sem, recv_sem, device):
        return pltpu.make_async_remote_copy(
            src_ref=source, dst_ref=target, send_sem=send_sem, recv_sem=recv_sem,
            device_id=device, device_id_type=MESH,
        )

    def swap(offset, a):
        blocks, everything = arrays[a]
        return remote(
            blocks.at[pair(offset)], everything.at[mine],
            swap_send.at[a, offset], swap_recv.at[a, offset], (rep, pair(offset)),
        )

    def far(hop, offset, a, block, place):
        return remote(
            block, place, far_send.at[hop - 1, a, offset], far_recv.at[hop - 1, a, offset],
            (ahead[hop], tp),
        )

    def near(hop, offset, a, block, place):
        return remote(
            block, place, near_send.at[hop, a, offset], near_recv.at[hop, a, offset],
            (partner, tp),
        )

    def place_of(group, offset, a):
        return arrays[a][1].at[group * tp_count + pair(offset)]

    def own(a):
        blocks, everything = arrays[a]
        return pltpu.make_async_copy(blocks.at[tp], everything.at[mine], own_sem.at[a])

    def spread(offset, a, block):
        place = place_of(rep, offset, a)
        for hop in hops:
            far(hop, offset, a, block, place).start()
        near(0, offset, a, block, place).start()

    def relay(offset, a):
        for hop in hops:
            place = place_of(behind[hop], offset, a)
            far(hop, offset, a, place, place).wait_recv()
            near(hop, offset, a, place, place).start()

    def collect(offset, a):
        for hop in (0, *hops):
            place = place_of(rep, offset, a)
            near(hop, offset, a, place, place).wait_recv()

        @pl.when(offset == 0)
        def _():
            own(a).wait()
            if multiply and a == 0:

                @pl.loop(0, count)
                def _(block):
                    load_probes(block).wait()


        if not multiply:
            return
        groups = [rep, partner]
        for hop in hops:
            groups += [behind[hop], across[hop]]
        tile, prints = ((query_tile, query_prints), (output_tile, output_prints))[a]
        loads = []
        for j, group in enumerate(groups):
            spot = (pl.ds(j * rows, rows), slice(None))
            load = pltpu.make_async_copy(
                place_of(group, offset, a), tile.at[spot if a == 0 else spot[::-1]],
                load_sem.at[a, j],
            )
            load.start()
            loads.append(load)
        for j, group in enumerate(groups):
            owner = owner_ref[group * tp_count + pair(offset)]
            picked[:, j * rows : (j + 1) * rows] = probes[owner]
        for load in loads:
            load.wait()
        if a == 0:
            prints[0] += jnp.dot(picked[...], tile[...], preferred_element_type=jnp.float32)
        else:
            prints[0] += lax.dot_general(
                tile[...], picked[...], (((1,), (1,)), ((), ())),
                preferred_element_type=jnp.float32,
            )

    for offset in range(1, tp_count):
        for a in range(2):
            swap(offset, a).start()
    for a in range(2):
        spread(jnp.int32(0), a, arrays[a][0].at[tp])
    for a in range(2):
        own(a).start()
    if multiply:

        @pl.loop(0, count)
        def _(block):
            load_probes(block).start()

        query_prints[...] = jnp.zeros_like(query_prints)
        output_prints[...] = jnp.zeros_like(output_prints)

    @pl.loop(1, tp_count + 2)
    def _(step):
        for a in range(2):

            @pl.when(step < tp_count)
            def _():
                swap(step, a).wait_recv()
                spread(step, a, place_of(rep, step, a))

            @pl.when(step <= tp_count)
            def _():
                relay(step - 1, a)

            if a == 0:

                @pl.when(step >= 2)
                def _():
                    collect(step - 2, 1)

            else:

                @pl.when(step <= tp_count)
                def _():
                    collect(step - 1, 0)

    @pl.loop(0, tp_count)
    def _(offset):
        for a in range(2):

            @pl.when(offset > 0)
            def _():
                swap(offset, a).wait_send()

            place = place_of(rep, offset, a)
            for hop in hops:
                far(hop, offset, a, place, place).wait_send()
            for hop in (0, *hops):
                near(hop, offset, a, place, place).wait_send()


def move(query_blocks, output_blocks, probes, shard_block, rep_count, multiply):
    tp_count, rows, cut = query_blocks.shape
    count = rep_count * tp_count
    half = rep_count // 2
    kinds = probes.shape[0]
    dma = pltpu.SemaphoreType.DMA
    anywhere = pl.BlockSpec(memory_space=pl.ANY)
    shapes = [
        jax.ShapeDtypeStruct((count, rows, cut), jnp.bfloat16),
        jax.ShapeDtypeStruct((count, cut, rows), jnp.bfloat16),
    ]
    scratch = [
        dma((2, tp_count)), dma((2, tp_count)),
        dma((half, 2, tp_count)), dma((half, 2, tp_count)),
        dma((half - 1, 2, tp_count)), dma((half - 1, 2, tp_count)),
        dma((2,)),
    ]
    operands, in_specs, out_specs = [query_blocks, output_blocks], [anywhere] * 2, [anywhere] * 2
    if multiply:
        operands = [shard_block] + operands + [probes]
        in_specs = [pl.BlockSpec(memory_space=pltpu.SMEM)] + [anywhere] * 3
        out_specs += [pl.BlockSpec(memory_space=pltpu.VMEM)] * 2
        shapes += [
            jax.ShapeDtypeStruct((1, kinds, cut), jnp.float32),
            jax.ShapeDtypeStruct((1, cut, kinds), jnp.float32),
        ]
        scratch += [
            pltpu.VMEM((count, kinds, rows), jnp.bfloat16),
            pltpu.VMEM((kinds, rep_count * rows), jnp.bfloat16),
            pltpu.VMEM((rep_count * rows, cut), jnp.bfloat16),
            pltpu.VMEM((cut, rep_count * rows), jnp.bfloat16),
            dma((2, rep_count)),
            dma((count,)),
        ]
    return pl.pallas_call(
        functools.partial(move_kernel, rep_count, tp_count, multiply),
        out_shape=shapes,
        in_specs=in_specs,
        out_specs=out_specs,
        scratch_shapes=scratch,
        compiler_params=pltpu.CompilerParams(collective_id=0, has_side_effects=True),
    )(*operands)


def order_kernel(group, inverse_ref, *refs):
    queries, outputs = refs[:group], refs[group : 2 * group]
    query_slice, output_slice = refs[2 * group :]
    rows = queries[0].shape[1]
    for j in range(group):
        query_slice[0, j * rows : (j + 1) * rows, :] = queries[j][0]
        output_slice[0, :, j * rows : (j + 1) * rows] = outputs[j][0]


def order(query_all, output_all, inverse):
    count, rows, cut = query_all.shape
    group = max(1, min(count, 1024 // rows))
    picks = range(group)
    return pl.pallas_call(
        functools.partial(order_kernel, group),
        out_shape=(
            jax.ShapeDtypeStruct((1, count * rows, cut), jnp.bfloat16),
            jax.ShapeDtypeStruct((1, cut, count * rows), jnp.bfloat16),
        ),
        grid_spec=pltpu.PrefetchScalarGridSpec(
            num_scalar_prefetch=1,
            grid=(count // group,),
            in_specs=[
                pl.BlockSpec((1, rows, cut), lambda b, inv, j=j: (inv[b * group + j], 0, 0))
                for j in picks
            ]
            + [
                pl.BlockSpec((1, cut, rows), lambda b, inv, j=j: (inv[b * group + j], 0, 0))
                for j in picks
            ],
            out_specs=[
                pl.BlockSpec((1, group * rows, cut), lambda b, inv: (0, b, 0)),
                pl.BlockSpec((1, cut, group * rows), lambda b, inv: (0, 0, b)),
            ],
        ),
    )(inverse, *([query_all] * group), *([output_all] * group))


def query_kernel(group, inverse_ref, *refs):
    blocks, (probes_ref, slice_ref, prints_ref) = refs[:group], refs[group:]
    rows = blocks[0].shape[1]
    for j, block in enumerate(blocks):
        slice_ref[0, j * rows : (j + 1) * rows, :] = block[0]
    part = jnp.dot(probes_ref[...], slice_ref[0], preferred_element_type=jnp.float32)

    @pl.when(pl.program_id(0) == 0)
    def _():
        prints_ref[0] = part

    @pl.when(pl.program_id(0) > 0)
    def _():
        prints_ref[0] += part


def output_kernel(group, inverse_ref, *refs):
    blocks, (probes_ref, slice_ref, prints_ref) = refs[:group], refs[group:]
    rows = blocks[0].shape[2]
    for j, block in enumerate(blocks):
        slice_ref[0, :, j * rows : (j + 1) * rows] = block[0]
    part = lax.dot_general(
        slice_ref[0], probes_ref[...], (((1,), (1,)), ((), ())),
        preferred_element_type=jnp.float32,
    )

    @pl.when(pl.program_id(0) == 0)
    def _():
        prints_ref[0] = part

    @pl.when(pl.program_id(0) > 0)
    def _():
        prints_ref[0] += part


def finish(body, everything, probes, inverse, slice_shape, prints_shape, along):
    count = everything.shape[0]
    block = everything.shape[1:]
    group = max(1, min(count, 1024 // block[along]))
    span = group * block[along]
    tile = list((1,) + block)
    tile[1 + along] = span
    in_specs = [
        pl.BlockSpec((1,) + block, lambda b, inv, j=j: (inv[b * group + j], 0, 0))
        for j in range(group)
    ]
    in_specs.append(pl.BlockSpec((probes.shape[0], span), lambda b, inv: (0, b)))
    place = (lambda b, inv: (0, b, 0)) if along == 0 else (lambda b, inv: (0, 0, b))
    return pl.pallas_call(
        functools.partial(body, group),
        out_shape=(
            jax.ShapeDtypeStruct(slice_shape, jnp.bfloat16),
            jax.ShapeDtypeStruct(prints_shape, jnp.float32),
        ),
        grid_spec=pltpu.PrefetchScalarGridSpec(
            num_scalar_prefetch=1,
            grid=(count // group,),
            in_specs=in_specs,
            out_specs=[
                pl.BlockSpec(tuple(tile), place),
                pl.BlockSpec(prints_shape, lambda b, inv: (0, 0, 0)),
            ],
        ),
    )(inverse, *([everything] * group), probes)


def per_device(trainer_query, trainer_output, probes, shard_block, slice_owner):
    tp_count = lax.axis_size("tp")
    rep_count = lax.axis_size("rep")
    count = tp_count * rep_count
    rows, width = trainer_query.shape[1:]
    cut = width // tp_count
    model = rows * count
    positions = jnp.arange(count, dtype=jnp.int32)
    held = shard_block[None, :] == positions[:, None]
    inverse = jnp.sum(jnp.where(held, positions[None, :], 0), axis=1, dtype=jnp.int32)
    query_blocks, output_blocks = pack(trainer_query, trainer_output, slice_owner)
    multiply = rows % 128 == 0
    moved = move(query_blocks, output_blocks, probes, shard_block, rep_count, multiply)
    if multiply:
        query_all, output_all, query_prints, output_prints = moved
        query_slice, output_slice = order(query_all, output_all, inverse)
        return query_slice, output_slice, query_prints, output_prints
    query_all, output_all = moved
    query_slice, query_prints = finish(
        query_kernel, query_all, probes, inverse,
        (1, model, cut), (1, probes.shape[0], cut), 0,
    )
    output_slice, output_prints = finish(
        output_kernel, output_all, probes, inverse,
        (1, cut, model), (1, cut, probes.shape[0]), 1,
    )
    return query_slice, output_slice, query_prints, output_prints


def solution(mesh):
    placed = (P(("rep", "tp"), None, None), P(("rep", "tp"), None, None), P(), P(), P())
    return jax.shard_map(
        per_device,
        mesh=mesh,
        in_specs=placed,
        out_specs=(
            P("tp", None, None),
            P("tp", None, None),
            P("tp", None, None),
            P("tp", None, None),
        ),
        check_vma=False,
    )
```

profile of v0, /device:TPU:0, one launch (start us, length us, event | category | flops | bytes accessed | tf_op | source)
XLA Modules:
  0.0 254.2 jit_solution(7599716230293266581)
XLA Ops:
  0.6 1.3 select_reduce_fusion.inverse_ref
  1.9 11.4 %shard_map.84 = (bf16[8,256,1024]{2,1,0:T(8,128)(2,1)}, bf16[8,1024,256]{2,1,0:T(8,128)(2,1)}) custom-call(s32[8]{0:T(128)} %owner_ref.1, f32[1,256,8192]{2,1,0:T(8,128)} %query_ref.1, f32[1,8192,256]{2,1,0:T(8,128)} %output_ref.1), custom_call_target="tpu_custom_call" | custom-call | tf_op jit(solution)/shard_map/pallas_call | solution.py:22
  13.4 212.4 %shard_map.85 = (bf16[32,256,1024]{2,1,0:T(8,128)(2,1)}, bf16[32,1024,256]{2,1,0:T(8,128)(2,1)}, f32[1,768,1024]{2,1,0:T(8,128)}, f32[1,1024,768]{2,1,0:T(8,128)}) custom-call(s32[32]{0:T(128)} %refs_0_.1, bf16[8,256,1024]{2,1,0:T(8,128)(2,1)} %get-tuple-element.12.refs_1_, bf16[8,1024,256]{2,1,0:T(8,128)(2,1)} %get-tuple-element.13.refs_2_, ...), custom_call_target="tpu_custom_call" | custom-call | tf_op jit(solution)/shard_map/pallas_call | solution.py:265
  225.7 0.0 copy-start.1
  225.7 23.8 %shard_map.86 = (bf16[1,8192,1024]{2,1,0:T(8,128)(2,1)}, bf16[1,1024,8192]{2,1,0:T(8,128)(2,1)}) custom-call(s32[32]{0:T(128)} %select_reduce_fusion.inverse_ref, bf16[32,256,1024]{2,1,0:T(8,128)(2,1)} %get-tuple-element.14.refs_0_.refs_1_.refs_2_.refs_3_, bf16[32,256,1024]{2,1,0:T(8,128)(2,1)} %get-tuple-element.14.refs_0_.refs_1_.refs_2_.refs_3_, ...), custom_call_target="tpu_custom_call" | custom-call | tf_op jit(solution)/shard_map/pallas_call | solution.py:288
  249.5 0.0 copy-start
  249.5 0.0 copy-done.1
  249.5 1.7 copy.11
  251.2 1.3 copy-done
  252.5 1.7 copy.12
Async XLA Ops:
  225.7 23.8 %copy-start.1 = (f32[1,768,1024]{2,1,0:T(8,128)S(1)}, f32[1,768,1024]{2,1,0:T(8,128)}, u32[]{:S(2)}) copy-start(f32[1,768,1024]{2,1,0:T(8,128)} %get-tuple-element.26) | copy-start | bytes 9437188
  249.5 3.0 %copy-start = (f32[1,1024,768]{2,1,0:T(8,128)S(1)}, f32[1,1024,768]{2,1,0:T(8,128)}, u32[]{:S(2)}) copy-start(f32[1,1024,768]{2,1,0:T(8,128)} %get-tuple-element.27) | copy-start | bytes 9437188
where the time goes:
time: 255 us; the launch traced here: 254 us
  Pallas kernels  248 us (97%)
  local copies, waits for them, and re-layouts  4.68 us (2%)
    pallas_call x1, Pallas kernels, move(): pl.pallas_call(functools.partial(move_kernel, rep_count, tp_count, multip...  212 us
    pallas_call x1, Pallas kernels, order(): pl.pallas_call(functools.partial(order_kernel, group), out_shape=(jax.Sha...  23.8 us
    pallas_call x1, Pallas kernels, pack(): pl.pallas_call(pack_kernel, out_shape=(jax.ShapeDtypeStruct((tp_count, ro...  11.4 us

commit v1 on v0

--- a/solution.py
+++ b/solution.py
@@ -8,6 +8,7 @@
 from jax.sharding import PartitionSpec as P
 
 MESH = pl.DeviceIdType.MESH
+VMEM_LIMIT = 99 * 256 * 1024
 
 
 def pack_kernel(owner_ref, query_ref, output_ref, query_blocks, output_blocks):
@@ -376,6 +377,364 @@
     )(inverse, *([everything] * group), probes)
 
 
+def stream_kernel(shard_ref, owner_ref, query_ref, output_ref, probes_ref,
+                  query_all, output_all, query_prints, output_prints,
+                  stage_even, stage_odd, query_out, output_out, probes, picked, query_tile, output_tile,
+                  stage_sem, probes_sem, swap_send, swap_recv, far_send, far_recv,
+                  near_send, near_recv):
+    rep_count, tp_count = lax.axis_size("rep"), lax.axis_size("tp")
+    rep, tp = lax.axis_index("rep"), lax.axis_index("tp")
+    count, rows, cut = query_all.shape
+    half = tp_count // 2
+    parts = cut // stage_even.shape[2]
+    size = stage_even.shape[2]
+    partner = rep + 1 - 2 * lax.rem(rep, 2)
+    facing = lax.rem(rep + 2, rep_count)
+    behind = facing + 1 - 2 * lax.rem(facing, 2)
+    mine = rep * tp_count + tp
+    inner = lax.rem(lax.div(lax.div(tp, 2) + 1, 2), 2)
+    everything = (query_all, output_all)
+    stage = (stage_even, stage_odd)
+    outgoing = (query_out, output_out)
+    ticks = half * parts
+
+    def pair(offset):
+        return pair_index(tp, jnp.int32(offset), tp_count)
+
+    def spot(a, part):
+        piece = pl.ds(pl.multiple_of(part * size, size), size)
+        return (slice(None), piece) if a == 0 else (piece, slice(None))
+
+    def remote(source, target, send_sem, recv_sem, device):
+        return pltpu.make_async_remote_copy(
+            src_ref=source, dst_ref=target, send_sem=send_sem, recv_sem=recv_sem,
+            device_id=device, device_id_type=MESH,
+        )
+
+    def swap(a, offset, part):
+        return remote(
+            outgoing[a].at[(offset - 1, *spot(a, part))],
+            everything[a].at[(mine, *spot(a, part))],
+            swap_send.at[a], swap_recv.at[a, offset, part], (rep, pair(offset)),
+        )
+
+    def held(group, a, offset, part):
+        return everything[a].at[(group * tp_count + pair(offset), *spot(a, part))]
+
+    def far(a, offset, part):
+        place = held(rep, a, offset, part)
+        return remote(place, place, far_send.at[a], far_recv.at[a, offset, part], (facing, tp))
+
+    def near(kind, a, offset, part):
+        place = held((rep, facing)[kind], a, offset, part)
+        return remote(
+            place, place, near_send.at[kind, a], near_recv.at[kind, a, offset, part],
+            (partner, tp),
+        )
+
+    def load(a, part, h):
+        copies = []
+        depth = size // 2
+        for k in range(tp_count):
+            if a == 0:
+                piece = pl.ds(pl.multiple_of(k * cut + part * size, size), size)
+                source = query_ref.at[0, h * rows // 2 : (h + 1) * rows // 2, piece]
+            else:
+                piece = pl.ds(pl.multiple_of(k * cut + part * size + h * depth, depth), depth)
+                source = output_ref.at[0, piece, :]
+            copies.append(pltpu.make_async_copy(source, stage[h].at[k], stage_sem.at[h, k]))
+        return copies
+
+    def start_load(a, part, h):
+        for copy in load(a, part, h):
+            copy.start()
+
+    def convert(part):
+        for a in range(2):
+            for h in range(2):
+                for copy in load(a, part, h):
+                    copy.wait()
+                if a == 0:
+                    piece = pl.ds(pl.multiple_of(part * size, size), size)
+                    where = (slice(h * rows // 2, (h + 1) * rows // 2), piece)
+                else:
+                    depth = size // 2
+                    piece = pl.ds(pl.multiple_of(part * size + h * depth, depth), depth)
+                    where = (piece, slice(None))
+                everything[a][(mine, *where)] = stage[h][owner_ref[tp]].astype(jnp.bfloat16)
+
+                @pl.loop(1, tp_count)
+                def _(offset):
+                    outgoing[a][(offset - 1, *where)] = stage[h][
+                        owner_ref[pair(offset)]
+                    ].astype(jnp.bfloat16)
+
+                if a == 0:
+                    start_load(1, part, h)
+                else:
+
+                    @pl.when(part < parts - 1)
+                    def _():
+                        start_load(0, part + 1, h)
+
+    def far_offset(e):
+        return half + 2 * lax.rem(lax.div(e, 2) + inner, 2) + lax.rem(e, 2)
+
+    def spread(a, offset, part):
+        far(a, offset, part).start()
+        near(0, a, offset, part).start()
+
+    def send_near(part):
+        @pl.loop(1, half)
+        def _(offset):
+            for a in range(2):
+                swap(a, offset, part).start()
+
+    def send_far(part):
+        @pl.loop(0, half)
+        def _(e):
+            for a in range(2):
+                swap(a, far_offset(e), part).start()
+
+    def item(p):
+        late = lax.div(p, 2 * ticks - half)
+        begun = lax.div(p + 2 * ticks - half, 2 * ticks)
+        mm = lax.div(p + half, 2) - half
+        b = lax.rem(p, 2)
+        is_far = begun * ((1 - late) * (1 - b) + late)
+        fm = late * (p - ticks) + (1 - late) * mm
+        fm = fm * is_far
+        near_part = begun * lax.div(mm + half, half)
+        near_offset = (1 - begun) * p + begun * lax.rem(mm + half, half)
+        offset = is_far * far_offset(lax.rem(fm, half)) + (1 - is_far) * near_offset
+        part = is_far * lax.div(fm, half) + (1 - is_far) * near_part
+        return offset, part
+
+    def relay(p):
+        offset, part = item(p)
+        for a in range(2):
+            far(a, offset, part).wait_recv()
+            near(1, a, offset, part).start()
+
+    def collect(p):
+        offset, part = item(p)
+        groups = (rep, partner, facing, behind)
+        for a in range(2):
+            for kind in range(2):
+                near(kind, a, offset, part).wait_recv()
+        for g, group in enumerate(groups):
+            source = group * tp_count + pair(offset)
+            strip = slice(g * rows, (g + 1) * rows)
+            picked[:, strip] = probes[shard_ref[source]]
+            query_tile[strip, :] = query_all[(source, *spot(0, part))]
+            output_tile[:, strip] = output_all[(source, *spot(1, part))]
+        query_prints[(0, *spot(0, part))] += jnp.dot(
+            picked[...], query_tile[...], preferred_element_type=jnp.float32
+        )
+        output_prints[(0, *spot(1, part))] += lax.dot_general(
+            output_tile[...], picked[...], (((1,), (1,)), ((), ())),
+            preferred_element_type=jnp.float32,
+        )
+
+    def load_probes(block):
+        columns = pl.ds(pl.multiple_of(block * rows, rows), rows)
+        return pltpu.make_async_copy(
+            probes_ref.at[:, columns], probes.at[block], probes_sem.at[block]
+        )
+
+    for h in range(2):
+        start_load(0, 0, h)
+    barrier = pltpu.get_barrier_semaphore()
+    peers = [(rep, pair(offset)) for offset in range(1, tp_count)]
+    peers += [(partner, tp), (facing, tp)]
+    for peer in peers:
+        pl.semaphore_signal(barrier, inc=1, device_id=peer, device_id_type=MESH)
+    convert(jnp.int32(0))
+    pl.semaphore_wait(barrier, len(peers))
+
+    for a in range(2):
+        spread(a, jnp.int32(0), 0)
+
+    @pl.when(inner == 1)
+    def _():
+        send_far(0)
+
+    send_near(0)
+    convert(jnp.int32(1))
+    send_near(1)
+
+    @pl.when(inner == 0)
+    def _():
+        send_far(0)
+
+    @pl.loop(0, count)
+    def _(block):
+        load_probes(block).start()
+
+    query_prints[...] = jnp.zeros_like(query_prints)
+    output_prints[...] = jnp.zeros_like(output_prints)
+
+    @pl.loop(1, half)
+    def _(offset):
+        for a in range(2):
+            swap(a, offset, 0).wait_recv()
+            spread(a, offset, 0)
+
+    @pl.loop(0, count)
+    def _(block):
+        load_probes(block).wait()
+
+    @pl.loop(0, ticks + 2)
+    def _(m):
+        @pl.loop(0, 2)
+        def _(i):
+            p = 2 * m - 3 + i
+
+            @pl.when((p >= 0) & (p < 2 * ticks))
+            def _():
+                collect(p)
+
+        q = lax.div(m, half)
+        j = lax.rem(m, half)
+
+        @pl.when(m < ticks)
+        def _():
+            offset = far_offset(j)
+            for a in range(2):
+                swap(a, offset, q).wait_recv()
+                spread(a, offset, q)
+
+        @pl.when(m < ticks - half)
+        def _():
+            @pl.when(j > 0)
+            def _():
+                for a in range(2):
+                    swap(a, j, q + 1).wait_recv()
+
+            for a in range(2):
+                spread(a, j, q + 1)
+
+            @pl.when((j == 1) & (q < parts - 2))
+            def _():
+                convert(q + 2)
+
+            @pl.when(j == 2)
+            def _():
+                @pl.when(inner == 1)
+                def _():
+                    send_far(q + 1)
+
+                @pl.when(q < parts - 2)
+                def _():
+                    send_near(q + 2)
+
+                @pl.when(inner == 0)
+                def _():
+                    send_far(q + 1)
+
+        @pl.loop(0, 2)
+        def _(i):
+            p = 2 * m - 1 + i
+
+            @pl.when((p >= 0) & (p < 2 * ticks))
+            def _():
+                relay(p)
+
+    for a in range(2):
+        whole = outgoing[a]
+        remote(whole, whole, swap_send.at[a], swap_recv.at[a, 0, 0], (partner, tp)).wait_send()
+        whole = everything[a].at[pl.ds(0, tp_count)]
+        for sem in (far_send.at[a], near_send.at[0, a], near_send.at[1, a]):
+            remote(whole, whole, sem, swap_recv.at[a, 0, 0], (partner, tp)).wait_send()
+
+
+def stream(trainer_query, trainer_output, probes, shard_block, slice_owner, rep_count):
+    tp_count = slice_owner.shape[0]
+    _, rows, width = trainer_query.shape
+    cut = width // tp_count
+    count = rep_count * tp_count
+    kinds = probes.shape[0]
+    parts = 4
+    size = cut // parts
+    dma = pltpu.SemaphoreType.DMA
+    anywhere = pl.BlockSpec(memory_space=pl.ANY)
+    small = pl.BlockSpec(memory_space=pltpu.SMEM)
+    depth = rep_count * rows
+    return pl.pallas_call(
+        stream_kernel,
+        out_shape=[
+            pltpu.VMEM((count, rows, cut), jnp.bfloat16),
+            pltpu.VMEM((count, cut, rows), jnp.bfloat16),
+            pltpu.VMEM((1, kinds, cut), jnp.float32),
+            pltpu.VMEM((1, cut, kinds), jnp.float32),
+        ],
+        in_specs=[small, small, anywhere, anywhere, anywhere],
+        out_specs=[pl.BlockSpec(memory_space=pltpu.VMEM)] * 4,
+        scratch_shapes=[
+            pltpu.VMEM((tp_count, size // 2, size), jnp.float32),
+            pltpu.VMEM((tp_count, size // 2, size), jnp.float32),
+            pltpu.VMEM((tp_count - 1, rows, cut), jnp.bfloat16),
+            pltpu.VMEM((tp_count - 1, cut, rows), jnp.bfloat16),
+            pltpu.VMEM((count, kinds, rows), jnp.bfloat16),
+            pltpu.VMEM((kinds, depth), jnp.bfloat16),
+            pltpu.VMEM((depth, size), jnp.bfloat16),
+            pltpu.VMEM((size, depth), jnp.bfloat16),
+            dma((2, tp_count)), dma((count,)),
+            dma((2,)), dma((2, tp_count, parts)),
+            dma((2,)), dma((2, tp_count, parts)),
+            dma((2, 2)), dma((2, 2, tp_count, parts)),
+        ],
+        compiler_params=pltpu.CompilerParams(
+            collective_id=0, has_side_effects=True, vmem_limit_bytes=VMEM_LIMIT
+        ),
+    )(shard_block, slice_owner, trainer_query, trainer_output, probes)
+
+
+def place_kernel(shard_ref, query_all, output_all, query_prints, output_prints,
+                 query_slice, output_slice, query_result, output_result, sems):
+    count, rows, _ = query_all.shape
+
+    @pl.loop(0, count)
+    def _(source):
+        block = pl.ds(pl.multiple_of(shard_ref[source] * rows, rows), rows)
+        pltpu.make_async_copy(
+            query_all.at[source], query_slice.at[0, block, :], sems.at[0]
+        ).start()
+        pltpu.make_async_copy(
+            output_all.at[source], output_slice.at[0, :, block], sems.at[1]
+        ).start()
+
+    prints = (
+        pltpu.make_async_copy(query_prints, query_result, sems.at[2]),
+        pltpu.make_async_copy(output_prints, output_result, sems.at[3]),
+    )
+    for copy in prints:
+        copy.start()
+    for k, everything in enumerate((query_all, output_all)):
+        pltpu.make_async_copy(everything, everything, sems.at[k]).wait()
+    for copy in prints:
+        copy.wait()
+
+
+def place(moved, shard_block):
+    query_all, output_all, query_prints, output_prints = moved
+    count, rows, cut = query_all.shape
+    inside = pl.BlockSpec(memory_space=pltpu.VMEM)
+    return pl.pallas_call(
+        place_kernel,
+        out_shape=(
+            jax.ShapeDtypeStruct((1, count * rows, cut), jnp.bfloat16),
+            jax.ShapeDtypeStruct((1, cut, count * rows), jnp.bfloat16),
+            jax.ShapeDtypeStruct(query_prints.shape, jnp.float32),
+            jax.ShapeDtypeStruct(output_prints.shape, jnp.float32),
+        ),
+        in_specs=[pl.BlockSpec(memory_space=pltpu.SMEM)] + [inside] * 4,
+        out_specs=[pl.BlockSpec(memory_space=pl.ANY)] * 4,
+        scratch_shapes=[pltpu.SemaphoreType.DMA((4,))],
+        compiler_params=pltpu.CompilerParams(vmem_limit_bytes=VMEM_LIMIT),
+    )(shard_block, *(pltpu.with_memory_space_constraint(x, pltpu.VMEM) for x in moved))
+
+
 def per_device(trainer_query, trainer_output, probes, shard_block, slice_owner):
     tp_count = lax.axis_size("tp")
     rep_count = lax.axis_size("rep")
@@ -383,6 +742,11 @@
     rows, width = trainer_query.shape[1:]
     cut = width // tp_count
     model = rows * count
+    if rep_count == 4 and tp_count == 8 and rows % 128 == 0 and cut == 4 * rows:
+        moved = stream(
+            trainer_query, trainer_output, probes, shard_block, slice_owner, rep_count
+        )
+        return place(moved, shard_block)
     positions = jnp.arange(count, dtype=jnp.int32)
     held = shard_block[None, :] == positions[:, None]
     inverse = jnp.sum(jnp.where(held, positions[None, :], 0), axis=1, dtype=jnp.int32)

time: 255 us -> 255 us (level)
  Pallas kernels: 248 us -> 254 us
  local copies, waits for them, and re-layouts: 4.68 us -> 0 us
    pallas_call x3 -> x2, Pallas kernels: 248 us -> 254 us  [the longest x1 240 us: stream(): pl.pallas_call(stream_kernel, out_shape=[pltpu.VMEM((count, rows, cut), j...]
    unnamed x6 -> x0, local copies, waits for them, and re-layouts: 4.68 us -> none
where the time goes in v1:
time: 255 us; the launch traced here: 254 us
  Pallas kernels  254 us (100%)
    pallas_call x1, Pallas kernels, stream(): pl.pallas_call(stream_kernel, out_shape=[pltpu.VMEM((count, rows, cut), j...  240 us
    pallas_call x1, Pallas kernels, place(): pl.pallas_call(place_kernel, out_shape=(jax.ShapeDtypeStruct((1, count *...  13.5 us

profile of v1, /device:TPU:0, one launch (start us, length us, event | category | flops | bytes accessed | tf_op | source)
XLA Modules:
  0.0 254.4 jit_solution(12567367414144450095)
XLA Ops:
  0.6 240.2 %shard_map.84 = (bf16[32,256,1024]{2,1,0:T(8,128)(2,1)S(1)}, bf16[32,1024,256]{2,1,0:T(8,128)(2,1)S(1)}, f32[1,768,1024]{2,1,0:T(8,128)S(1)}, f32[1,1024,768]{2,1,0:T(8,128)S(1)}) custom-call(s32[32]{0:T(128)} %shard_ref.3, s32[8]{0:T(128)} %owner_ref.1, f32[1,256,8192]{2,1,0:T(8,128)} %query_ref.1, f32[1,8192,256]{2,1,0:T(8,128)} %output_ref.1, ...), custom_call_target="tpu_custom_call" | custom-call | tf_op jit(solution)/shard_map/pallas_call | solution.py:663
  240.9 13.5 %shard_map.85 = (bf16[1,8192,1024]{2,1,0:T(8,128)(2,1)}, bf16[1,1024,8192]{2,1,0:T(8,128)(2,1)}, f32[1,768,1024]{2,1,0:T(8,128)}, f32[1,1024,768]{2,1,0:T(8,128)}) custom-call(s32[32]{0:T(128)} %shard_ref.3, bf16[32,256,1024]{2,1,0:T(8,128)(2,1)S(1)} %get-tuple-element.8.query_all, bf16[32,1024,256]{2,1,0:T(8,128)(2,1)S(1)} %get-tuple-element.9.output_all, ...), custom_call_target="tpu_custom_call" | custom-call | tf_op jit(solution)/shard_map/pallas_call | solution.py:723

commit v2 on v1

--- a/solution.py
+++ b/solution.py
@@ -9,6 +9,8 @@
 
 MESH = pl.DeviceIdType.MESH
 VMEM_LIMIT = 99 * 256 * 1024
+LEAD = 3
+LAG = 1
 
 
 def pack_kernel(owner_ref, query_ref, output_ref, query_blocks, output_blocks):
@@ -397,6 +399,7 @@
     stage = (stage_even, stage_odd)
     outgoing = (query_out, output_out)
     ticks = half * parts
+    first = half + 1
 
     def pair(offset):
         return pair_index(tp, jnp.int32(offset), tp_count)
@@ -449,8 +452,8 @@
         for copy in load(a, part, h):
             copy.start()
 
-    def convert(part):
-        for a in range(2):
+    def convert(a, part):
+        if True:
             for h in range(2):
                 for copy in load(a, part, h):
                     copy.wait()
@@ -478,37 +481,36 @@
                         start_load(0, part + 1, h)
 
     def far_offset(e):
-        return half + 2 * lax.rem(lax.div(e, 2) + inner, 2) + lax.rem(e, 2)
+        return half + 2 * (1 - lax.rem(e, 2)) + lax.div(e, 2)
 
     def spread(a, offset, part):
         far(a, offset, part).start()
         near(0, a, offset, part).start()
 
-    def send_near(part):
+    def send_near(a, part):
         @pl.loop(1, half)
         def _(offset):
-            for a in range(2):
-                swap(a, offset, part).start()
-
-    def send_far(part):
-        @pl.loop(0, half)
-        def _(e):
-            for a in range(2):
-                swap(a, far_offset(e), part).start()
+            swap(a, offset, part).start()
+
+    def send_far(a, n):
+        swap(a, far_offset(lax.rem(n, half)), lax.div(n, half)).start()
+
+    def near_item(k):
+        shifted = k + half - 1 + lax.div(k, 3 * half + 1)
+        j = lax.rem(shifted, half)
+        part = lax.div(shifted, half) - lax.min(j, 1)
+        return j * lax.min(k, 1), lax.max(part, 0)
 
     def item(p):
-        late = lax.div(p, 2 * ticks - half)
-        begun = lax.div(p + 2 * ticks - half, 2 * ticks)
-        mm = lax.div(p + half, 2) - half
-        b = lax.rem(p, 2)
-        is_far = begun * ((1 - late) * (1 - b) + late)
-        fm = late * (p - ticks) + (1 - late) * mm
-        fm = fm * is_far
-        near_part = begun * lax.div(mm + half, half)
-        near_offset = (1 - begun) * p + begun * lax.rem(mm + half, half)
-        offset = is_far * far_offset(lax.rem(fm, half)) + (1 - is_far) * near_offset
-        part = is_far * lax.div(fm, half) + (1 - is_far) * near_part
-        return offset, part
+        late = lax.div(p, 2 * ticks - first)
+        begun = lax.div(p + 2 * ticks - first, 2 * ticks)
+        middle = lax.div(p + 2 * half - first, 2) - half
+        is_far = begun * (late + (1 - late) * lax.rem(p, 2))
+        n = is_far * (late * (p - ticks) + (1 - late) * middle)
+        k = (1 - is_far) * (begun * (first + middle) + (1 - begun) * p)
+        near_offset, near_part = near_item(k)
+        offset = is_far * far_offset(lax.rem(n, half)) + (1 - is_far) * near_offset
+        return offset, is_far * lax.div(n, half) + (1 - is_far) * near_part
 
     def relay(p):
         offset, part = item(p)
@@ -549,23 +551,28 @@
     peers += [(partner, tp), (facing, tp)]
     for peer in peers:
         pl.semaphore_signal(barrier, inc=1, device_id=peer, device_id_type=MESH)
-    convert(jnp.int32(0))
-    pl.semaphore_wait(barrier, len(peers))
-
     for a in range(2):
+        convert(a, jnp.int32(0))
+        if a == 0:
+            pl.semaphore_wait(barrier, len(peers))
         spread(a, jnp.int32(0), 0)
 
-    @pl.when(inner == 1)
-    def _():
-        send_far(0)
-
-    send_near(0)
-    convert(jnp.int32(1))
-    send_near(1)
-
-    @pl.when(inner == 0)
-    def _():
-        send_far(0)
+        @pl.when(inner == 1)
+        def _():
+            for n in range(LEAD):
+                send_far(a, jnp.int32(n))
+
+        send_near(a, 0)
+
+        @pl.when(inner == 0)
+        def _():
+            for n in range(LEAD):
+                send_far(a, jnp.int32(n))
+
+    for a in range(2):
+        convert(a, jnp.int32(1))
+        spread(a, jnp.int32(0), 1)
+        send_near(a, 1)
 
     @pl.loop(0, count)
     def _(block):
@@ -573,6 +580,8 @@
 
     query_prints[...] = jnp.zeros_like(query_prints)
     output_prints[...] = jnp.zeros_like(output_prints)
+    for a in range(2):
+        convert(a, jnp.int32(2))
 
     @pl.loop(1, half)
     def _(offset):
@@ -584,57 +593,52 @@
     def _(block):
         load_probes(block).wait()
 
-    @pl.loop(0, ticks + 2)
+    @pl.loop(0, ticks + 2 + LAG)
     def _(m):
         @pl.loop(0, 2)
         def _(i):
-            p = 2 * m - 3 + i
+            p = 2 * (m - LAG) - 3 + i
 
             @pl.when((p >= 0) & (p < 2 * ticks))
             def _():
                 collect(p)
 
-        q = lax.div(m, half)
-        j = lax.rem(m, half)
-
         @pl.when(m < ticks)
         def _():
-            offset = far_offset(j)
+            offset, part = far_offset(lax.rem(m, half)), lax.div(m, half)
             for a in range(2):
-                swap(a, offset, q).wait_recv()
-                spread(a, offset, q)
-
-        @pl.when(m < ticks - half)
-        def _():
-            @pl.when(j > 0)
+                swap(a, offset, part).wait_recv()
+                spread(a, offset, part)
+
+            @pl.when(m < ticks - LEAD)
             def _():
                 for a in range(2):
-                    swap(a, j, q + 1).wait_recv()
-
+                    send_far(a, m + LEAD)
+
+        @pl.when(m < ticks - first)
+        def _():
+            offset, part = near_item(first + m)
             for a in range(2):
-                spread(a, j, q + 1)
-
-            @pl.when((j == 1) & (q < parts - 2))
-            def _():
-                convert(q + 2)
-
-            @pl.when(j == 2)
-            def _():
-                @pl.when(inner == 1)
+
+                @pl.when(offset > 0)
                 def _():
-                    send_far(q + 1)
-
-                @pl.when(q < parts - 2)
-                def _():
-                    send_near(q + 2)
-
-                @pl.when(inner == 0)
-                def _():
-                    send_far(q + 1)
+                    swap(a, lax.max(offset, 1), part).wait_recv()
+
+                spread(a, offset, part)
+
+        @pl.when(m == 0)
+        def _():
+            for a in range(2):
+                convert(a, jnp.int32(parts - 1))
+
+        @pl.when((m == 1) | (m == half))
+        def _():
+            for a in range(2):
+                send_near(a, 2 + lax.div(m, half))
 
         @pl.loop(0, 2)
         def _(i):
-            p = 2 * m - 1 + i
+            p = 2 * (m - LAG) - 1 + i
 
             @pl.when((p >= 0) & (p < 2 * ticks))
             def _():

time: 255 us -> 217 us (0.85)
  Pallas kernels: 254 us -> 215 us
    pallas_call x1, Pallas kernels: 240 us -> 202 us  [stream(): pl.pallas_call(stream_kernel, out_shape=[pltpu.VMEM((count, rows, cut), j...]
where the time goes in v2:
time: 217 us; the launch traced here: 216 us
  Pallas kernels  215 us (99%)
    pallas_call x1, Pallas kernels, stream(): pl.pallas_call(stream_kernel, out_shape=[pltpu.VMEM((count, rows, cut), j...  202 us
    pallas_call x1, Pallas kernels, place(): pl.pallas_call(place_kernel, out_shape=(jax.ShapeDtypeStruct((1, count *...  13.5 us

profile of v2, /device:TPU:0, one launch (start us, length us, event | category | flops | bytes accessed | tf_op | source)
XLA Modules:
  0.0 215.9 jit_solution(10961943232077536052)
XLA Ops:
  0.6 201.8 %shard_map.84 = (bf16[32,256,1024]{2,1,0:T(8,128)(2,1)S(1)}, bf16[32,1024,256]{2,1,0:T(8,128)(2,1)S(1)}, f32[1,768,1024]{2,1,0:T(8,128)S(1)}, f32[1,1024,768]{2,1,0:T(8,128)S(1)}) custom-call(s32[32]{0:T(128)} %shard_ref.3, s32[8]{0:T(128)} %owner_ref.1, f32[1,256,8192]{2,1,0:T(8,128)} %query_ref.1, f32[1,8192,256]{2,1,0:T(8,128)} %output_ref.1, ...), custom_call_target="tpu_custom_call" | custom-call | tf_op jit(solution)/shard_map/pallas_call | solution.py:667
  202.4 13.5 %shard_map.85 = (bf16[1,8192,1024]{2,1,0:T(8,128)(2,1)}, bf16[1,1024,8192]{2,1,0:T(8,128)(2,1)}, f32[1,768,1024]{2,1,0:T(8,128)}, f32[1,1024,768]{2,1,0:T(8,128)}) custom-call(s32[32]{0:T(128)} %shard_ref.3, bf16[32,256,1024]{2,1,0:T(8,128)(2,1)S(1)} %get-tuple-element.8.query_all, bf16[32,1024,256]{2,1,0:T(8,128)(2,1)S(1)} %get-tuple-element.9.output_all, ...), custom_call_target="tpu_custom_call" | custom-call | tf_op jit(solution)/shard_map/pallas_call | solution.py:727

commit v3 on v2

--- a/solution.py
+++ b/solution.py
@@ -8,8 +8,8 @@
 from jax.sharding import PartitionSpec as P
 
 MESH = pl.DeviceIdType.MESH
-VMEM_LIMIT = 99 * 256 * 1024
-LEAD = 3
+VMEM_LIMIT = 51 * 256 * 1024
+LEAD = 6
 LAG = 1
 
 
@@ -380,16 +380,18 @@
 
 
 def stream_kernel(shard_ref, owner_ref, query_ref, output_ref, probes_ref,
-                  query_all, output_all, query_prints, output_prints,
-                  stage_even, stage_odd, query_out, output_out, probes, picked, query_tile, output_tile,
+                  query_all, output_all, query_prints, output_prints, probes,
+                  stage_even, stage_odd, query_out, output_out, picked, query_tile, output_tile,
                   stage_sem, probes_sem, swap_send, swap_recv, far_send, far_recv,
                   near_send, near_recv):
     rep_count, tp_count = lax.axis_size("rep"), lax.axis_size("tp")
     rep, tp = lax.axis_index("rep"), lax.axis_index("tp")
     count, rows, cut = query_all.shape
     half = tp_count // 2
-    parts = cut // stage_even.shape[2]
     size = stage_even.shape[2]
+    strips = cut // size
+    step = size // 2
+    parts = cut // step
     partner = rep + 1 - 2 * lax.rem(rep, 2)
     facing = lax.rem(rep + 2, rep_count)
     behind = facing + 1 - 2 * lax.rem(facing, 2)
@@ -399,12 +401,12 @@
     stage = (stage_even, stage_odd)
     outgoing = (query_out, output_out)
     ticks = half * parts
-    first = half + 1
+    first = half + 2 * (half - 1)
 
     def pair(offset):
         return pair_index(tp, jnp.int32(offset), tp_count)
 
-    def spot(a, part):
+    def spot(a, part, size=step):
         piece = pl.ds(pl.multiple_of(part * size, size), size)
         return (slice(None), piece) if a == 0 else (piece, slice(None))
 
@@ -476,7 +478,7 @@
                     start_load(1, part, h)
                 else:
 
-                    @pl.when(part < parts - 1)
+                    @pl.when(part < strips - 1)
                     def _():
                         start_load(0, part + 1, h)
 
@@ -496,16 +498,23 @@
         swap(a, far_offset(lax.rem(n, half)), lax.div(n, half)).start()
 
     def near_item(k):
-        shifted = k + half - 1 + lax.div(k, 3 * half + 1)
-        j = lax.rem(shifted, half)
-        part = lax.div(shifted, half) - lax.min(j, 1)
-        return j * lax.min(k, 1), lax.max(part, 0)
+        begun = lax.min(lax.div(k, half), 1)
+        middle = lax.min(lax.div(k, first), 1)
+        last = lax.min(lax.div(k, first + 4 * half), 1)
+        j = lax.rem(k + 2, half)
+        offset = (begun - middle) * (lax.rem(k + 2, half - 1) + 1)
+        offset += (middle - last) * j
+        offset += last * (lax.rem(k + 1, half - 1) + 1)
+        part = (1 - begun) * k + (begun - middle) * (lax.div(k + 2, half - 1) - 2)
+        part += (middle - last) * (lax.div(k + 2, half) + 1 - 2 * lax.min(j, 1))
+        part += last * (lax.div(k + 1, half - 1) - 3)
+        return offset, part
 
     def item(p):
         late = lax.div(p, 2 * ticks - first)
         begun = lax.div(p + 2 * ticks - first, 2 * ticks)
-        middle = lax.div(p + 2 * half - first, 2) - half
-        is_far = begun * (late + (1 - late) * lax.rem(p, 2))
+        middle = lax.div(p + first, 2) - first
+        is_far = begun * (late + (1 - late) * (1 - lax.rem(p, 2)))
         n = is_far * (late * (p - ticks) + (1 - late) * middle)
         k = (1 - is_far) * (begun * (first + middle) + (1 - begun) * p)
         near_offset, near_part = near_item(k)
@@ -524,19 +533,23 @@
         for a in range(2):
             for kind in range(2):
                 near(kind, a, offset, part).wait_recv()
-        for g, group in enumerate(groups):
-            source = group * tp_count + pair(offset)
-            strip = slice(g * rows, (g + 1) * rows)
-            picked[:, strip] = probes[shard_ref[source]]
-            query_tile[strip, :] = query_all[(source, *spot(0, part))]
-            output_tile[:, strip] = output_all[(source, *spot(1, part))]
-        query_prints[(0, *spot(0, part))] += jnp.dot(
-            picked[...], query_tile[...], preferred_element_type=jnp.float32
-        )
-        output_prints[(0, *spot(1, part))] += lax.dot_general(
-            output_tile[...], picked[...], (((1,), (1,)), ((), ())),
-            preferred_element_type=jnp.float32,
-        )
+
+        @pl.when((lax.rem(part, 2) == 1) & (p < 2 * ticks - half))
+        def _():
+            strip = lax.div(part, 2)
+            for g, group in enumerate(groups):
+                source = group * tp_count + pair(offset)
+                along = slice(g * rows, (g + 1) * rows)
+                picked[:, along] = probes[shard_ref[source]]
+                query_tile[along, :] = query_all[(source, *spot(0, strip, size))]
+                output_tile[:, along] = output_all[(source, *spot(1, strip, size))]
+            query_prints[(0, *spot(0, strip, size))] += jnp.dot(
+                picked[...], query_tile[...], preferred_element_type=jnp.float32
+            )
+            output_prints[(0, *spot(1, strip, size))] += lax.dot_general(
+                output_tile[...], picked[...], (((1,), (1,)), ((), ())),
+                preferred_element_type=jnp.float32,
+            )
 
     def load_probes(block):
         columns = pl.ds(pl.multiple_of(block * rows, rows), rows)
@@ -555,14 +568,16 @@
         convert(a, jnp.int32(0))
         if a == 0:
             pl.semaphore_wait(barrier, len(peers))
-        spread(a, jnp.int32(0), 0)
+        for part in range(2):
+            spread(a, jnp.int32(0), part)
 
         @pl.when(inner == 1)
         def _():
             for n in range(LEAD):
                 send_far(a, jnp.int32(n))
 
-        send_near(a, 0)
+        for part in range(2):
+            send_near(a, part)
 
         @pl.when(inner == 0)
         def _():
@@ -571,8 +586,9 @@
 
     for a in range(2):
         convert(a, jnp.int32(1))
-        spread(a, jnp.int32(0), 1)
-        send_near(a, 1)
+        for part in range(2, 4):
+            spread(a, jnp.int32(0), part)
+        send_near(a, 2)
 
     @pl.loop(0, count)
     def _(block):
@@ -583,11 +599,12 @@
     for a in range(2):
         convert(a, jnp.int32(2))
 
-    @pl.loop(1, half)
-    def _(offset):
+    @pl.loop(half, first)
+    def _(k):
+        offset, part = near_item(k)
         for a in range(2):
-            swap(a, offset, 0).wait_recv()
-            spread(a, offset, 0)
+            swap(a, offset, part).wait_recv()
+            spread(a, offset, part)
 
     @pl.loop(0, count)
     def _(block):
@@ -626,15 +643,15 @@
 
                 spread(a, offset, part)
 
-        @pl.when(m == 0)
+        @pl.when(m == 1)
         def _():
             for a in range(2):
-                convert(a, jnp.int32(parts - 1))
-
-        @pl.when((m == 1) | (m == half))
+                convert(a, jnp.int32(strips - 1))
+
+        @pl.when((lax.rem(m, 3) == 0) & (m < 3 * (parts - 3)))
         def _():
             for a in range(2):
-                send_near(a, 2 + lax.div(m, half))
+                send_near(a, 3 + lax.div(m, 3))
 
         @pl.loop(0, 2)
         def _(i):
@@ -658,8 +675,8 @@
     cut = width // tp_count
     count = rep_count * tp_count
     kinds = probes.shape[0]
-    parts = 4
-    size = cut // parts
+    size = cut // 4
+    parts = 8
     dma = pltpu.SemaphoreType.DMA
     anywhere = pl.BlockSpec(memory_space=pl.ANY)
     small = pl.BlockSpec(memory_space=pltpu.SMEM)
@@ -671,15 +688,15 @@
             pltpu.VMEM((count, cut, rows), jnp.bfloat16),
             pltpu.VMEM((1, kinds, cut), jnp.float32),
             pltpu.VMEM((1, cut, kinds), jnp.float32),
+            pltpu.VMEM((count, kinds, rows), jnp.bfloat16),
         ],
         in_specs=[small, small, anywhere, anywhere, anywhere],
-        out_specs=[pl.BlockSpec(memory_space=pltpu.VMEM)] * 4,
+        out_specs=[pl.BlockSpec(memory_space=pltpu.VMEM)] * 5,
         scratch_shapes=[
             pltpu.VMEM((tp_count, size // 2, size), jnp.float32),
             pltpu.VMEM((tp_count, size // 2, size), jnp.float32),
             pltpu.VMEM((tp_count - 1, rows, cut), jnp.bfloat16),
             pltpu.VMEM((tp_count - 1, cut, rows), jnp.bfloat16),
-            pltpu.VMEM((count, kinds, rows), jnp.bfloat16),
             pltpu.VMEM((kinds, depth), jnp.bfloat16),
             pltpu.VMEM((depth, size), jnp.bfloat16),
             pltpu.VMEM((size, depth), jnp.bfloat16),
@@ -694,9 +711,14 @@
     )(shard_block, slice_owner, trainer_query, trainer_output, probes)
 
 
-def place_kernel(shard_ref, query_all, output_all, query_prints, output_prints,
-                 query_slice, output_slice, query_result, output_result, sems):
-    count, rows, _ = query_all.shape
+def place_kernel(shard_ref, query_all, output_all, query_prints, output_prints, probes,
+                 query_slice, output_slice, query_result, output_result,
+                 query_last, output_last, picked, query_tile, output_tile, sems):
+    rep_count, tp_count = lax.axis_size("rep"), lax.axis_size("tp")
+    tp = lax.axis_index("tp")
+    count, rows, cut = query_all.shape
+    size = query_tile.shape[1]
+    early, late = slice(0, cut - size), slice(cut - size, cut)
 
     @pl.loop(0, count)
     def _(source):
@@ -708,11 +730,40 @@
             output_all.at[source], output_slice.at[0, :, block], sems.at[1]
         ).start()
 
-    prints = (
-        pltpu.make_async_copy(query_prints, query_result, sems.at[2]),
-        pltpu.make_async_copy(output_prints, output_result, sems.at[3]),
-    )
+    prints = [
+        pltpu.make_async_copy(
+            query_prints.at[0, :, early], query_result.at[0, :, early], sems.at[2]
+        ),
+        pltpu.make_async_copy(
+            output_prints.at[0, early, :], output_result.at[0, early, :], sems.at[3]
+        ),
+    ]
     for copy in prints:
+        copy.start()
+    query_last[...] = query_prints[0, :, late]
+    output_last[...] = output_prints[0, late, :]
+
+    @pl.loop(tp_count // 2, tp_count)
+    def _(offset):
+        for g in range(rep_count):
+            source = g * tp_count + pair_index(tp, offset, tp_count)
+            along = slice(g * rows, (g + 1) * rows)
+            picked[:, along] = probes[shard_ref[source]]
+            query_tile[along, :] = query_all[source, :, late]
+            output_tile[:, along] = output_all[source, late, :]
+        query_last[...] += jnp.dot(
+            picked[...], query_tile[...], preferred_element_type=jnp.float32
+        )
+        output_last[...] += lax.dot_general(
+            output_tile[...], picked[...], (((1,), (1,)), ((), ())),
+            preferred_element_type=jnp.float32,
+        )
+
+    prints += [
+        pltpu.make_async_copy(query_last, query_result.at[0, :, late], sems.at[4]),
+        pltpu.make_async_copy(output_last, output_result.at[0, late, :], sems.at[5]),
+    ]
+    for copy in prints[2:]:
         copy.start()
     for k, everything in enumerate((query_all, output_all)):
         pltpu.make_async_copy(everything, everything, sems.at[k]).wait()
@@ -721,8 +772,11 @@
 
 
 def place(moved, shard_block):
-    query_all, output_all, query_prints, output_prints = moved
+    query_all, output_all, query_prints, output_prints, probes = moved
     count, rows, cut = query_all.shape
+    kinds = probes.shape[1]
+    size = cut // 4
+    depth = lax.axis_size("rep") * rows
     inside = pl.BlockSpec(memory_space=pltpu.VMEM)
     return pl.pallas_call(
         place_kernel,
@@ -732,9 +786,16 @@
             jax.ShapeDtypeStruct(query_prints.shape, jnp.float32),
             jax.ShapeDtypeStruct(output_prints.shape, jnp.float32),
         ),
-        in_specs=[pl.BlockSpec(memory_space=pltpu.SMEM)] + [inside] * 4,
+        in_specs=[pl.BlockSpec(memory_space=pltpu.SMEM)] + [inside] * 5,
         out_specs=[pl.BlockSpec(memory_space=pl.ANY)] * 4,
-        scratch_shapes=[pltpu.SemaphoreType.DMA((4,))],
+        scratch_shapes=[
+            pltpu.VMEM((kinds, size), jnp.float32),
+            pltpu.VMEM((size, kinds), jnp.float32),
+            pltpu.VMEM((kinds, depth), jnp.bfloat16),
+            pltpu.VMEM((depth, size), jnp.bfloat16),
+            pltpu.VMEM((size, depth), jnp.bfloat16),
+            pltpu.SemaphoreType.DMA((6,)),
+        ],
         compiler_params=pltpu.CompilerParams(vmem_limit_bytes=VMEM_LIMIT),
     )(shard_block, *(pltpu.with_memory_space_constraint(x, pltpu.VMEM) for x in moved))
 

time: 217 us -> 215 us (level)
  no operation moved by 1% of the time
where the time goes in v3:
time: 215 us; the launch traced here: 214 us
  Pallas kernels  214 us (100%)
    pallas_call x1, Pallas kernels, stream(): pl.pallas_call(stream_kernel, out_shape=[pltpu.VMEM((count, rows, cut), j...  200 us
    pallas_call x1, Pallas kernels, place(): pl.pallas_call(place_kernel, out_shape=(jax.ShapeDtypeStruct((1, count *...  13.5 us

profile of v3, /device:TPU:0, one launch (start us, length us, event | category | flops | bytes accessed | tf_op | source)
XLA Modules:
  0.0 214.3 jit_solution(10054904479605998960)
XLA Ops:
  0.6 200.2 %shard_map.84 = (bf16[32,256,1024]{2,1,0:T(8,128)(2,1)S(1)}, bf16[32,1024,256]{2,1,0:T(8,128)(2,1)S(1)}, f32[1,768,1024]{2,1,0:T(8,128)S(1)}, f32[1,1024,768]{2,1,0:T(8,128)S(1)}, bf16[32,768,256]{2,1,0:T(8,128)(2,1)S(1)}) custom-call(s32[32]{0:T(128)} %shard_ref.3, s32[8]{0:T(128)} %owner_ref.1, f32[1,256,8192]{2,1,0:T(8,128)} %query_ref.1, ...), custom_call_target="tpu_custom_call" | custom-call | tf_op jit(solution)/shard_map/pallas_call | solution.py:684
  200.8 13.5 %shard_map.85 = (bf16[1,8192,1024]{2,1,0:T(8,128)(2,1)}, bf16[1,1024,8192]{2,1,0:T(8,128)(2,1)}, f32[1,768,1024]{2,1,0:T(8,128)}, f32[1,1024,768]{2,1,0:T(8,128)}) custom-call(s32[32]{0:T(128)} %shard_ref.3, bf16[32,256,1024]{2,1,0:T(8,128)(2,1)S(1)} %get-tuple-element.9.query_all, bf16[32,1024,256]{2,1,0:T(8,128)(2,1)S(1)} %get-tuple-element.10.output_all, ...), custom_call_target="tpu_custom_call" | custom-call | tf_op jit(solution)/shard_map/pallas_call | solution.py:781
